TPU v7x, 8 devices: a whole 2x2x1 slice. The times are simulated.
8 devices in a mesh: dp: 1 (over z), ep: 8 (over y, x, core).
Axes of the slice: x: 2, y: 2, z: 1, core: 2. Of those that a mesh axis runs over, the one named last changes fastest.
Arguments:
- x: bfloat16 [768, 2048], P(('dp', 'ep'))
- route_idx: int32 [768, 6], P(('dp', 'ep'))
- gates: float32 [768, 6], P(('dp', 'ep'))
- w_gate: bfloat16 [64, 2048, 1408], P('ep')
- w_up: bfloat16 [64, 2048, 1408], P('ep')
- w_down: bfloat16 [64, 1408, 2048], P('ep')
- shared_gate: bfloat16 [2048, 2816], replicated
- shared_up: bfloat16 [2048, 2816], replicated
- shared_down: bfloat16 [2816, 2048], replicated
Outputs:
- output: bfloat16 [768, 2048], P(('dp', 'ep'))
All inputs are finite; a program needn't handle non-finite values.
Results may differ from a plain program's by a relative error of at most 0.00804522.
Values are sent between devices in bfloat16 or wider.
A program may use at most 1 GiB of HBM per device.

v0:
```python
import functools

import jax
import jax.numpy as jnp
from jax import lax
from jax.experimental import pallas as pl
from jax.experimental.pallas import tpu as pltpu
from jax.sharding import PartitionSpec as P

MESH = pl.DeviceIdType.MESH
CAP = 36
SLOT = 40
VMEM_LIMIT = 67_000_000
H_BYTES = 8_000_000
PRE = 2
PRE_BYTES = 23_500_000
BF16 = jnp.bfloat16
F32 = jnp.float32


def neighbours():
    me = lax.axis_index("ep")
    core = me % 2
    xb = (me // 2) % 2
    yb = me // 4
    sib = me + 1 - 2 * core
    xn = me + 2 - 4 * xb
    yn = me + 4 - 8 * yb
    dg = yn + 2 - 4 * xb
    return me, core, sib, xn, yn, dg


def rcopy(src, dst, send, recv, dev):
    return pltpu.make_async_remote_copy(
        src_ref=src, dst_ref=dst, send_sem=send, recv_sem=recv,
        device_id={"ep": dev}, device_id_type=MESH)


def gather_kernel(x_ref, route_ref, gate_ref, sg_hbm, su_hbm, w1_hbm, w3_hbm,
                  xg_hbm, hsh_hbm, cnt_hbm, g_hbm, pre1, pre3,
                  land, meta_s, bg, bu, metal, stage, hsh, gv, cntv,
                  wsem, osem, psem, gsem, hsem, csem,
                  sx_s, sx_r, sy_s, sy_r, f_s, f_r, ss_s, ss_r, m_s, m_r):
    me, core, sib, xn, yn, dg = neighbours()
    sxn = xn + 1 - 2 * core
    syn = yn + 1 - 2 * core
    sdg = dg + 1 - 2 * core
    nd = land.shape[0]
    rows, d_model = x_ref.shape
    half = rows // 2
    ring = bg.shape[0]
    width = bg.shape[2]
    n_chunks = sg_hbm.shape[1] // width
    n_all = 8 * nd

    barrier = pltpu.get_barrier_semaphore()
    for r in range(1, nd):
        pl.semaphore_signal(barrier, inc=1, device_id={"ep": (me + r) % nd}, device_id_type=MESH)

    def wcopy(i):
        cols = pl.ds(pl.multiple_of(i * width, width), width)
        slot = i % ring
        return (pltpu.make_async_copy(sg_hbm.at[:, cols], bg.at[slot], wsem.at[0, slot]),
                pltpu.make_async_copy(su_hbm.at[:, cols], bu.at[slot], wsem.at[1, slot]))

    for i in range(ring):
        for c in wcopy(i):
            c.start()

    def pcopy(e):
        return (pltpu.make_async_copy(w1_hbm.at[e], pre1.at[e], psem.at[0, e]),
                pltpu.make_async_copy(w3_hbm.at[e], pre3.at[e], psem.at[1, e]))

    def prefetch(e):
        for c in pcopy(e):
            c.start()

    ids = lax.broadcasted_iota(jnp.int32, (n_all, rows), 0)
    mask = jnp.zeros((n_all, rows), F32)
    gmap = jnp.zeros((n_all, rows), F32)
    for k in range(route_ref.shape[0]):
        eq = route_ref[k:k + 1, :] == ids
        mask = mask + jnp.where(eq, 1.0, 0.0)
        gmap = gmap + jnp.where(eq, gate_ref[k:k + 1, :], 0.0)
    before = (lax.broadcasted_iota(jnp.int32, (rows, rows), 0)
              < lax.broadcasted_iota(jnp.int32, (rows, rows), 1))
    rank = jnp.dot(mask.astype(BF16), jnp.where(before, 1.0, 0.0).astype(BF16), preferred_element_type=F32)
    rank = jnp.where(mask > 0.0, rank, -1.0)
    fill = jnp.zeros((n_all, 128 - rows), F32)
    rank = jnp.concatenate([rank, fill - 1.0], axis=1)
    gmap = jnp.concatenate([gmap, fill], axis=1)
    for j in range(nd):
        meta_s[j, 0:8, :] = rank[8 * j:8 * j + 8]
        meta_s[j, 8:16, :] = gmap[8 * j:8 * j + 8]
    metal[me] = meta_s[me]

    def hs(h):
        return pl.ds(h * half, half)

    pl.semaphore_wait(barrier, nd - 1)
    metas = []
    for r in range(1, nd):
        dst = (me + r) % nd
        c = rcopy(meta_s.at[dst], metal.at[me], m_s.at[r - 1], m_r.at[r - 1], dst)
        c.start()
        metas.append(c)
    own_x = [rcopy(x_ref.at[hs(h)], land.at[me, hs(h)], sx_s.at[h], sx_r.at[h], xn) for h in range(2)]
    own_y = [rcopy(x_ref.at[hs(h)], land.at[me, hs(h)], sy_s.at[h], sy_r.at[h], yn) for h in range(2)]
    own_s = rcopy(x_ref, land.at[me], ss_s.at[0], ss_r.at[0], sib)
    own_x[0].start()
    own_y[1].start()
    own_x[1].start()
    own_y[0].start()
    own_s.start()

    def shared_range(lo, hi):
        def body(i, carry):
            for c in wcopy(i):
                c.wait()
            a = jnp.dot(x_ref[...], bg[i % ring], preferred_element_type=F32)
            b = jnp.dot(x_ref[...], bu[i % ring], preferred_element_type=F32)
            cols = pl.ds(pl.multiple_of(i * width, width), width)
            hsh[:, cols] = (jax.nn.silu(a) * b).astype(BF16)

            @pl.when(i + ring < n_chunks)
            def _():
                for c in wcopy(i + ring):
                    c.start()
            return carry
        lax.fori_loop(lo, hi, body, 0)

    shared_range(0, 2)
    prefetch(0)
    shared_range(2, n_chunks - 5)
    prefetch(1)

    for c in metas:
        c.wait_recv()

    for d in range(nd):
        n = jnp.sum(jnp.where(metal[d, 0:8, :] >= 0.0, 1.0, 0.0), axis=1, keepdims=True)
        cntv[d] = jnp.broadcast_to(n, (8, 128)).astype(jnp.int32)
    ccopy = pltpu.make_async_copy(cntv, cnt_hbm, csem)
    ccopy.start()

    def pick(d, x_rows, k):
        buf = k % 2
        if k >= 2:
            outs[k - 2].wait()
        slot = lax.broadcasted_iota(jnp.int32, (SLOT, rows), 0).astype(F32)
        sel = jnp.concatenate(
            [jnp.where(metal[d, e:e + 1, 0:rows] == slot, 1.0, 0.0) for e in range(8)], axis=0).astype(BF16)
        for c0 in range(0, d_model, 512):
            r = jnp.dot(sel, x_rows[:, c0:c0 + 512], preferred_element_type=F32)
            stage[buf, :, :, c0:c0 + 512] = r.astype(BF16).reshape(8, SLOT, 512)
        c = pltpu.make_async_copy(stage.at[buf], xg_hbm.at[:, d], osem.at[k])
        c.start()
        outs.append(c)

    outs = []
    pick(me, x_ref, 0)
    own_s.wait_recv()
    pick(sib, land.at[sib], 1)

    own_x[0].wait_recv()
    fy = rcopy(land.at[xn, hs(0)], land.at[xn, hs(0)], f_s.at[0], f_r.at[0], yn)
    fy.start()
    sx0 = rcopy(land.at[xn, hs(0)], land.at[xn, hs(0)], ss_s.at[1], ss_r.at[1], sib)
    sx0.start()
    own_y[1].wait_recv()
    fx = rcopy(land.at[yn, hs(1)], land.at[yn, hs(1)], f_s.at[1], f_r.at[1], xn)
    fx.start()
    sy1 = rcopy(land.at[yn, hs(1)], land.at[yn, hs(1)], ss_s.at[2], ss_r.at[2], sib)
    sy1.start()

    shared_range(n_chunks - 5, n_chunks)
    for e in range(2, pre1.shape[0]):
        prefetch(e)
    hcopy = pltpu.make_async_copy(hsh, hsh_hbm, hsem)
    hcopy.start()

    own_x[1].wait_recv()
    sx1 = rcopy(land.at[xn, hs(1)], land.at[xn, hs(1)], ss_s.at[3], ss_r.at[3], sib)
    sx1.start()
    own_y[0].wait_recv()
    sy0 = rcopy(land.at[yn, hs(0)], land.at[yn, hs(0)], ss_s.at[4], ss_r.at[4], sib)
    sy0.start()
    pick(xn, land.at[xn], 2)
    pick(yn, land.at[yn], 3)
    sx0.wait_recv()
    sx1.wait_recv()
    pick(sxn, land.at[sxn], 4)
    sy1.wait_recv()
    sy0.wait_recv()
    pick(syn, land.at[syn], 5)

    width_g = 8 * SLOT
    lane = lax.broadcasted_iota(jnp.int32, (8, width_g), 1)
    sel = jnp.where(lane // SLOT == lax.broadcasted_iota(jnp.int32, (8, width_g), 0), 1.0, 0.0)
    slot_id = (lax.broadcasted_iota(jnp.int32, (rows, width_g), 1) % SLOT).astype(F32)

    def spread(v):
        return lax.dot_general(v, sel, (((0,), (0,)), ((), ())), preferred_element_type=F32)[:rows]

    def gate_body(d, carry):
        rk = metal[d, 0:8, :]
        gt = metal[d, 8:16, :]
        hi = gt.astype(BF16).astype(F32)
        mid = (gt - hi).astype(BF16).astype(F32)
        lo = gt - hi - mid
        eq = spread(rk) == slot_id
        for q, part in enumerate((hi, mid, lo)):
            gv[d, q * rows:(q + 1) * rows, :] = jnp.where(eq, spread(part), 0.0).astype(BF16)
        return carry

    lax.fori_loop(0, nd, gate_body, 0)
    gcopy = pltpu.make_async_copy(gv, g_hbm, gsem)
    gcopy.start()

    fy.wait_recv()
    sd0 = rcopy(land.at[dg, hs(0)], land.at[dg, hs(0)], ss_s.at[5], ss_r.at[5], sib)
    sd0.start()
    fx.wait_recv()
    sd1 = rcopy(land.at[dg, hs(1)], land.at[dg, hs(1)], ss_s.at[6], ss_r.at[6], sib)
    sd1.start()
    pick(dg, land.at[dg], 6)
    sd0.wait_recv()
    sd1.wait_recv()
    pick(sdg, land.at[sdg], 7)
    for c in own_x + own_y + [own_s, fy, fx, sx0, sx1, sy0, sy1, sd0, sd1] + metas:
        c.wait_send()
    for c in outs[6:] + [ccopy, hcopy, gcopy]:
        c.wait()
    for e in range(pre1.shape[0]):
        for c in pcopy(e):
            c.wait()


def gather_call(x, route, gates, sg, su, w1, w3, nd):
    rows, d_model = x.shape
    ff = sg.shape[1]
    width = 256
    ring = 4
    any_spec = pl.BlockSpec(memory_space=pl.ANY)
    vmem = pl.BlockSpec(memory_space=pltpu.VMEM)
    dma = pltpu.SemaphoreType.DMA
    return pl.pallas_call(
        gather_kernel,
        out_shape=(
            jax.ShapeDtypeStruct((8, nd, SLOT, d_model), BF16),
            jax.ShapeDtypeStruct((rows, ff), BF16),
            jax.ShapeDtypeStruct((nd, 8, 128), jnp.int32),
            jax.ShapeDtypeStruct((nd, 3 * rows, 8 * SLOT), BF16),
            pltpu.VMEM((PRE,) + w1.shape[1:], BF16),
            pltpu.VMEM((PRE,) + w3.shape[1:], BF16),
        ),
        in_specs=[vmem, vmem, vmem] + [any_spec] * 4,
        out_specs=(pl.BlockSpec(memory_space=pltpu.HBM),) * 4 + (vmem, vmem),
        scratch_shapes=[
            pltpu.VMEM((nd, rows, d_model), BF16),
            pltpu.VMEM((nd, 16, 128), F32),
            pltpu.VMEM((ring, d_model, width), BF16),
            pltpu.VMEM((ring, d_model, width), BF16),
            pltpu.VMEM((nd, 16, 128), F32),
            pltpu.VMEM((2, 8, SLOT, d_model), BF16),
            pltpu.VMEM((rows, ff), BF16),
            pltpu.VMEM((nd, 3 * rows, 8 * SLOT), BF16),
            pltpu.VMEM((nd, 8, 128), jnp.int32),
            dma((2, ring)),
            dma((8,)), dma((2, PRE)), dma(()), dma(()), dma(()),
            dma((2,)), dma((2,)), dma((2,)), dma((2,)), dma((2,)), dma((2,)),
            dma((7,)), dma((7,)), dma((7,)), dma((7,)),
        ],
        compiler_params=pltpu.CompilerParams(
            collective_id=0, has_side_effects=True, vmem_limit_bytes=36_000_000),
        name="gather_shared",
    )(x, route, gates, sg, su, w1, w3)


FEW = 16


def hidden_kernel(cnt, xg_hbm, w1_hbm, w3_hbm, pre1, pre3, h_ref,
                  wb1, wb3, xfew, xall, wsem, xsem):
    n_exp, d_model, ff = w1_hbm.shape
    nd = cnt.shape[0]
    depth = wb1.shape[0]
    first = pre1.shape[0]
    bounds = [(c, min(256, ff - c)) for c in range(0, ff, 256)]
    cut = 3 * 256
    groups = ((0, cut, bounds[:3]), (cut, ff - cut, bounds[3:]))

    def wcopy(e, slot, j):
        c0, w, _ = groups[j]
        return (pltpu.make_async_copy(w1_hbm.at[e, :, c0:c0 + w], wb1.at[slot, :, c0:c0 + w], wsem.at[slot, 0, j]),
                pltpu.make_async_copy(w3_hbm.at[e, :, c0:c0 + w], wb3.at[slot, :, c0:c0 + w], wsem.at[slot, 1, j]))

    def few(e):
        top = cnt[0, e, 0]
        for d in range(1, nd):
            top = jnp.maximum(top, cnt[d, e, 0])
        return top <= FEW

    def few_copy(e):
        return pltpu.make_async_copy(xg_hbm.at[e, :, pl.ds(0, FEW)], xfew.at[e % 2], xsem.at[e % 2])

    def all_copy(e):
        return pltpu.make_async_copy(xg_hbm.at[e], xall.at[e % 2], xsem.at[e % 2])

    def rows_start(e):
        @pl.when(few(e))
        def _():
            few_copy(e).start()

        @pl.when(jnp.logical_not(few(e)))
        def _():
            all_copy(e).start()

    rows_start(0)
    rows_start(1)
    for e in range(first, first + depth):
        for j in range(len(groups)):
            for c in wcopy(e, e % depth, j):
                c.start()
    h_ref[...] = jnp.zeros_like(h_ref)

    def hidden(rows_ref, up, gate, c0, w):
        m = rows_ref.shape[0] * rows_ref.shape[1]
        a = jnp.dot(rows_ref[...].reshape(m, d_model), gate[:, c0:c0 + w], preferred_element_type=F32)
        b = jnp.dot(rows_ref[...].reshape(m, d_model), up[:, c0:c0 + w], preferred_element_type=F32)
        return (jax.nn.silu(a) * b).astype(BF16).reshape(rows_ref.shape[0], rows_ref.shape[1], w)

    def expert(e, gate, up, wait):
        small = few(e)

        @pl.when(small)
        def _():
            few_copy(e).wait()
            for j, (_, _, cols) in enumerate(groups):
                wait(j)
                for c0, w in cols:
                    h_ref[e, :, 0:FEW, c0:c0 + w] = hidden(xfew.at[e % 2], up, gate, c0, w)

        @pl.when(jnp.logical_not(small))
        def _():
            all_copy(e).wait()
            for j, (_, _, cols) in enumerate(groups):
                wait(j)
                for c0, w in cols:
                    h_ref[e, :, :, c0:c0 + w] = hidden(xall.at[e % 2], up, gate, c0, w)

        @pl.when(e + 2 < n_exp)
        def _():
            rows_start(e + 2)

    def early(e, carry):
        expert(e, pre1.at[e], pre3.at[e], lambda j: None)
        return carry

    def late(e, carry):
        slot = e % depth

        def wait(j):
            for c in wcopy(e, slot, j):
                c.wait()

        expert(e, wb1.at[slot], wb3.at[slot], wait)

        @pl.when(e + depth < n_exp)
        def _():
            for j in range(len(groups)):
                for c in wcopy(e + depth, slot, j):
                    c.start()
        return carry

    lax.fori_loop(0, first, early, 0)
    lax.fori_loop(first, n_exp, late, 0)


def hidden_call(cnt, xg, w1, w3, pre1, pre3):
    n_exp, d_model, ff = w1.shape
    nd = cnt.shape[0]
    depth = 2
    any_spec = pl.BlockSpec(memory_space=pl.ANY)
    vmem = pl.BlockSpec(memory_space=pltpu.VMEM)
    dma = pltpu.SemaphoreType.DMA
    return pl.pallas_call(
        hidden_kernel,
        out_shape=pltpu.VMEM((n_exp, nd, SLOT, ff), BF16),
        in_specs=[pl.BlockSpec(memory_space=pltpu.SMEM), any_spec, any_spec, any_spec, vmem, vmem],
        out_specs=vmem,
        scratch_shapes=[
            pltpu.VMEM((depth, d_model, ff), BF16),
            pltpu.VMEM((depth, d_model, ff), BF16),
            pltpu.VMEM((2, nd, FEW, d_model), BF16),
            pltpu.VMEM((2, nd, SLOT, d_model), BF16),
            dma((depth, 2, 2)), dma((2,)),
        ],
        compiler_params=pltpu.CompilerParams(vmem_limit_bytes=36_000_000),
        name="routed_hidden",
    )(cnt, xg, w1, w3, pltpu.with_memory_space_constraint(pre1, pltpu.VMEM),
      pltpu.with_memory_space_constraint(pre3, pltpu.VMEM))


def down_kernel(hv, g_hbm, hsh_ref, w2_hbm, sd_hbm, y_ref,
                gv, wb, sdb, ob, snd, kept, in0, in1, in2,
                gsem, wsem, dsem, s0s, s0r, s1s, s1r, s2s, s2r):
    me, core, sib, xn, yn, dg = neighbours()
    n_exp, full, ff = hv.shape
    nd = gv.shape[0]
    rows = gv.shape[1] // 3
    n_chunks = snd.shape[0]
    width = wb.shape[3]
    depth = wb.shape[0]
    hw = width // 2

    barrier = pltpu.get_barrier_semaphore()
    for dev in (sib, xn, yn):
        pl.semaphore_signal(barrier, inc=1, device_id={"ep": dev}, device_id_type=MESH)

    def wcopy(c, e):
        cols = pl.ds(pl.multiple_of(c * width, width), width)
        slot = c % depth
        return pltpu.make_async_copy(w2_hbm.at[e, :, cols], wb.at[slot, e], wsem.at[slot, e])

    def dcopy(c):
        cols = pl.ds(pl.multiple_of(c * width, width), width)
        return pltpu.make_async_copy(sd_hbm.at[:, cols], sdb.at[c], dsem.at[c])

    gcopy = pltpu.make_async_copy(g_hbm, gv, gsem)
    for e in range(n_exp):
        wcopy(0, e).start()
    gcopy.start()
    for c in range(1, depth):
        for e in range(n_exp):
            wcopy(c, e).start()

    own_c, xn_c, yn_c, dg_c = me // 2, xn // 2, yn // 2, dg // 2
    orders = ((own_c, yn_c, xn_c, dg_c), (own_c, xn_c, yn_c, dg_c))
    first_hop = (xn, yn)
    second_hop = (yn, xn)

    def send0(c):
        return rcopy(snd.at[c], in0.at[c], s0s.at[c], s0r.at[c], sib)

    def send1(c, q):
        return rcopy(kept.at[c, q, pl.ds(2, 2)], in1.at[c, q], s1s.at[c, q], s1r.at[c, q], first_hop[q])

    def send2(c, q):
        return rcopy(kept.at[c, q, 1], in2.at[c, q], s2s.at[c, q], s2r.at[c, q], second_hop[q])

    def step0(c):
        send0(c).wait_recv()
        kept[c] = kept[c] + in0[c]

    def step1(c):
        for q in range(2):
            send1(c, q).wait_recv()
            kept[c, q, 0:2] = kept[c, q, 0:2] + in1[c, q]

    def step2(c):
        for q in range(2):
            send2(c, q).wait_recv()
            kept[c, q, 0] = kept[c, q, 0] + in2[c, q]

    def start1(c):
        send1(c, 0).start()
        send1(c, 1).start()

    def start2(c):
        send2(c, 0).start()
        send2(c, 1).start()

    def expert(c, e):
        out = jnp.dot(hv[e], wb[c % depth, e], preferred_element_type=F32)
        out = out.astype(BF16).astype(F32)
        ob[:, e] = out.reshape(nd, SLOT, width)

    def gated(d):
        o = ob[d].reshape(n_exp * SLOT, width).astype(BF16)
        r = jnp.dot(gv[d], o, preferred_element_type=F32)
        return r[0:rows] + r[rows:2 * rows] + r[2 * rows:3 * rows]

    def chunk(c, carry):
        for e0 in range(0, n_exp, 4):
            for e in range(e0, e0 + 4):
                wcopy(c, e).wait()
            for e in range(e0, e0 + 4):
                expert(c, e)

            @pl.when(c + depth < n_chunks)
            def _():
                for e in range(e0, e0 + 4):
                    wcopy(c + depth, e).start()

            if e0 == 0:
                @pl.when(c >= 1)
                def _():
                    step0(c - 1)

                @pl.when(c >= 3)
                def _():
                    step1(c - 3)

                @pl.when(c >= 1)
                def _():
                    start1(c - 1)

                @pl.when(c >= 3)
                def _():
                    start2(c - 3)

        dcopy(c).start()

        @pl.when(c == 0)
        def _():
            gcopy.wait()
        chips = (own_c, xn_c, yn_c, dg_c)
        where = ((0, 0), (2, 1), (1, 2), (3, 3))
        for chip, (p0, p1) in zip(chips, where):
            r = gated(2 * chip + 1 - core)
            snd[c, 0, p0] = r[:, 0:hw]
            snd[c, 1, p1] = r[:, hw:width]
        for chip, (p0, p1) in zip(chips, where):
            r = gated(2 * chip + core)
            kept[c, 0, p0] = r[:, 0:hw]
            kept[c, 1, p1] = r[:, hw:width]

        send0(c).start()
        return carry

    pl.semaphore_wait(barrier, 3)
    lax.fori_loop(0, n_chunks, chunk, 0)

    def shared(c):
        dcopy(c).wait()
        cols = pl.ds(pl.multiple_of(c * width, width), width)
        s = jnp.dot(hsh_ref[...], sdb[c], preferred_element_type=F32).astype(BF16)
        y_ref[:, cols] = s

    def shared_range(lo, hi):
        def body(c, carry):
            shared(c)
            return carry
        lax.fori_loop(lo, hi, body, 0)

    last = n_chunks - 1
    shared_range(0, 3)
    step0(last)
    step1(last - 2)
    start1(last)
    start2(last - 2)
    shared_range(3, 6)
    step1(last - 1)
    start2(last - 1)
    shared_range(6, n_chunks)
    step1(last)
    start2(last)

    def finish(c, carry):
        step2(c)
        for q in range(2):
            cols = pl.ds(pl.multiple_of(c * width + q * hw, hw), hw)
            y_ref[:, cols] = (y_ref[:, cols].astype(F32) + kept[c, q, 0]).astype(BF16)
        return carry

    lax.fori_loop(0, n_chunks, finish, 0)

    def drain(c, carry):
        send0(c).wait_send()
        for q in range(2):
            send1(c, q).wait_send()
            send2(c, q).wait_send()
        return carry

    lax.fori_loop(0, n_chunks, drain, 0)


def down_call(h, g, hsh, w2, sd):
    n_exp, full, ff = h.shape
    nd, rows3, width_g = g.shape
    rows = rows3 // 3
    d_model = w2.shape[2]
    width = 256
    n_chunks = d_model // width
    depth = 3
    hw = width // 2
    any_spec = pl.BlockSpec(memory_space=pl.ANY)
    vmem = pl.BlockSpec(memory_space=pltpu.VMEM)
    dma = pltpu.SemaphoreType.DMA
    return pl.pallas_call(
        down_kernel,
        out_shape=jax.ShapeDtypeStruct((rows, d_model), BF16),
        in_specs=[vmem, any_spec, vmem, any_spec, any_spec],
        out_specs=vmem,
        scratch_shapes=[
            pltpu.VMEM((nd, rows3, width_g), BF16),
            pltpu.VMEM((depth, n_exp, ff, width), BF16),
            pltpu.VMEM((n_chunks, sd.shape[0], width), BF16),
            pltpu.VMEM((nd, n_exp, SLOT, width), F32),
            pltpu.VMEM((n_chunks, 2, 4, rows, hw), F32),
            pltpu.VMEM((n_chunks, 2, 4, rows, hw), F32),
            pltpu.VMEM((n_chunks, 2, 4, rows, hw), F32),
            pltpu.VMEM((n_chunks, 2, 2, rows, hw), F32),
            pltpu.VMEM((n_chunks, 2, rows, hw), F32),
            dma(()), dma((depth, n_exp)), dma((n_chunks,)),
            dma((n_chunks,)), dma((n_chunks,)),
            dma((n_chunks, 2)), dma((n_chunks, 2)), dma((n_chunks, 2)), dma((n_chunks, 2)),
        ],
        compiler_params=pltpu.CompilerParams(
            collective_id=1, has_side_effects=True, vmem_limit_bytes=VMEM_LIMIT - H_BYTES),
        name="down_reduce",
    )(pltpu.with_memory_space_constraint(h, pltpu.VMEM), g, hsh, w2, sd)


def solution(mesh):
    nd = mesh.shape["ep"]

    def device_fn(x, route, gates, w_gate, w_up, w_down, sg, su, sd):
        xg, hsh, cnt, g, pre1, pre3 = gather_call(x, route.T, gates.T, sg, su, w_gate, w_up, nd)
        h = hidden_call(cnt, xg, w_gate, w_up, pre1, pre3)
        return down_call(h.reshape(h.shape[0], -1, h.shape[3]), g, hsh, w_down, sd)

    tok = P(("dp", "ep"), None)
    exp = P("ep", None, None)
    rep = P(None, None)
    return jax.shard_map(device_fn, mesh=mesh, in_specs=(tok, tok, tok, exp, exp, exp, rep, rep, rep),
                         out_specs=tok, check_vma=False)
```

profile of v0, /device:TPU:0, one launch (start us, length us, event | category | flops | bytes accessed | tf_op | source)
XLA Modules:
  0.0 108.5 jit_solution(13738882779616346575)
XLA Ops:
  0.0 27.7 %gather_shared.1 = (bf16[8,8,40,2048]{3,2,1,0:T(8,128)(2,1)}, bf16[96,2816]{1,0:T(8,128)(2,1)}, s32[8,8,128]{2,1,0:T(8,128)}, bf16[8,288,320]{2,1,0:T(8,128)(2,1...) custom-call(bf16[96,2048]{1,0:T(8,128)(2,1)} %x_ref.1, s32[6,96]{1,0:T(8,128)} %bitcast.4, ...), custom_call_target="tpu_custom_call" | custom-call | tf_op jit(solution)/shard_map/gather_shared/pallas_call | solution.py:247
  27.7 30.5 %routed_hidden.1 = bf16[8,8,40,1408]{3,2,1,0:T(8,128)(2,1)S(1)} custom-call(s32[8,8,128]{2,1,0:T(8,128)} %get-tuple-element.11.cnt, bf16[8,8,40,2048]{3,2,1,0:T(8,128)(2,1)} %get-tuple-element.12.xg_hbm, bf16[8,2048,1408]{2,1,0:T(8,128)(2,1)} %w1_hbm.3, bf16[8,2048,1408]{2,1,0:T(8,128)(2,1)} %w3_hbm.3, bf16[2,2048,1408]{2,1,0:T(8,128)(2,1)S(1)} %get-tuple-element.13.pre1, ...), custom_call_target="tpu_custom_call" | custom-call | tf_op jit(solution)/shard_map/routed_hidden/pallas_call | solution.py:387
  58.2 48.5 %down_reduce.1 = bf16[96,2048]{1,0:T(8,128)(2,1)} custom-call(bf16[8,320,1408]{2,1,0:T(8,128)(2,1)S(1)} %bitcast.3, bf16[8,288,320]{2,1,0:T(8,128)(2,1)} %get-tuple-element.15.g_hbm, bf16[96,2816]{1,0:T(8,128)(2,1)} %get-tuple-element.16.hsh_ref, bf16[8,1408,2048]{2,1,0:T(8,128)(2,1)} %w2_hbm.1, bf16[2816,2048]{1,0:T(8,128)(2,1)} %sd_hbm.1), custom_call_target="tpu_custom_call" | custom-call | tf_op jit(solution)/shard_map/down_reduce/pallas_call | solution.py:591
  106.8 1.8 %copy.11 = bf16[96,2048]{1,0:T(8,128)(2,1)} copy(bf16[96,2048]{1,0:T(8,128)(2,1)} %down_reduce.1) | data formatting | bytes 786432
where the time goes:
time: 108 us; the launch traced here: 109 us
  Pallas kernels  107 us (99%)
  local copies, waits for them, and re-layouts  1.77 us (2%)
    pallas_call x1, Pallas kernels, down_call(): pl.pallas_call(down_kernel, out_shape=jax.ShapeDtypeStruct((rows, d_model...  48.5 us
    pallas_call x1, Pallas kernels, hidden_call(): pl.pallas_call(hidden_kernel, out_shape=pltpu.VMEM((n_exp, nd, SLOT, ff),...  30.5 us
    pallas_call x1, Pallas kernels, gather_call(): pl.pallas_call(gather_kernel, out_shape=(jax.ShapeDtypeStruct((8, nd, SLO...  27.7 us

commit v1 on v0

--- a/solution.py
+++ b/solution.py
@@ -11,7 +11,9 @@
 CAP = 36
 SLOT = 40
 VMEM_LIMIT = 67_000_000
-H_BYTES = 8_000_000
+H_BYTES = 10_500_000
+CHUNK = 256
+EARLY = 2
 PRE = 2
 PRE_BYTES = 23_500_000
 BF16 = jnp.bfloat16
@@ -272,7 +274,7 @@
             dma((7,)), dma((7,)), dma((7,)), dma((7,)),
         ],
         compiler_params=pltpu.CompilerParams(
-            collective_id=0, has_side_effects=True, vmem_limit_bytes=36_000_000),
+            collective_id=0, has_side_effects=True, vmem_limit_bytes=33_800_000),
         name="gather_shared",
     )(x, route, gates, sg, su, w1, w3)
 
@@ -280,8 +282,8 @@
 FEW = 16
 
 
-def hidden_kernel(cnt, xg_hbm, w1_hbm, w3_hbm, pre1, pre3, h_ref,
-                  wb1, wb3, xfew, xall, wsem, xsem):
+def hidden_kernel(cnt, xg_hbm, w1_hbm, w3_hbm, w2_hbm, pre1, pre3, h_ref,
+                  wb1, wb3, wb2, xfew, xall, wsem, dsem, xsem):
     n_exp, d_model, ff = w1_hbm.shape
     nd = cnt.shape[0]
     depth = wb1.shape[0]
@@ -316,8 +318,15 @@
         def _():
             all_copy(e).start()
 
+    early_w = wb2.shape[2]
+
+    def dcopy(e):
+        return pltpu.make_async_copy(w2_hbm.at[e, :, pl.ds(0, early_w)], wb2.at[e % 2], dsem.at[e % 2])
+
     rows_start(0)
+    dcopy(0).start()
     rows_start(1)
+    dcopy(1).start()
     for e in range(first, first + depth):
         for j in range(len(groups)):
             for c in wcopy(e, e % depth, j):
@@ -329,6 +338,12 @@
         a = jnp.dot(rows_ref[...].reshape(m, d_model), gate[:, c0:c0 + w], preferred_element_type=F32)
         b = jnp.dot(rows_ref[...].reshape(m, d_model), up[:, c0:c0 + w], preferred_element_type=F32)
         return (jax.nn.silu(a) * b).astype(BF16).reshape(rows_ref.shape[0], rows_ref.shape[1], w)
+
+    def down(e, slots):
+        rows = h_ref[e, :, 0:slots, 0:ff].reshape(nd * slots, ff)
+        for c0 in range(0, early_w, 256):
+            out = jnp.dot(rows, wb2[e % 2, :, c0:c0 + 256], preferred_element_type=F32)
+            h_ref[e, :, 0:slots, ff + c0:ff + c0 + 256] = out.astype(BF16).reshape(nd, slots, 256)
 
     def expert(e, gate, up, wait):
         small = few(e)
@@ -340,6 +355,8 @@
                 wait(j)
                 for c0, w in cols:
                     h_ref[e, :, 0:FEW, c0:c0 + w] = hidden(xfew.at[e % 2], up, gate, c0, w)
+            dcopy(e).wait()
+            down(e, FEW)
 
         @pl.when(jnp.logical_not(small))
         def _():
@@ -348,10 +365,13 @@
                 wait(j)
                 for c0, w in cols:
                     h_ref[e, :, :, c0:c0 + w] = hidden(xall.at[e % 2], up, gate, c0, w)
+            dcopy(e).wait()
+            down(e, SLOT)
 
         @pl.when(e + 2 < n_exp)
         def _():
             rows_start(e + 2)
+            dcopy(e + 2).start()
 
     def early(e, carry):
         expert(e, pre1.at[e], pre3.at[e], lambda j: None)
@@ -377,7 +397,7 @@
     lax.fori_loop(first, n_exp, late, 0)
 
 
-def hidden_call(cnt, xg, w1, w3, pre1, pre3):
+def hidden_call(cnt, xg, w1, w3, w2, pre1, pre3):
     n_exp, d_model, ff = w1.shape
     nd = cnt.shape[0]
     depth = 2
@@ -386,19 +406,20 @@
     dma = pltpu.SemaphoreType.DMA
     return pl.pallas_call(
         hidden_kernel,
-        out_shape=pltpu.VMEM((n_exp, nd, SLOT, ff), BF16),
-        in_specs=[pl.BlockSpec(memory_space=pltpu.SMEM), any_spec, any_spec, any_spec, vmem, vmem],
+        out_shape=pltpu.VMEM((n_exp, nd, SLOT, ff + EARLY * CHUNK), BF16),
+        in_specs=[pl.BlockSpec(memory_space=pltpu.SMEM)] + [any_spec] * 4 + [vmem, vmem],
         out_specs=vmem,
         scratch_shapes=[
             pltpu.VMEM((depth, d_model, ff), BF16),
             pltpu.VMEM((depth, d_model, ff), BF16),
+            pltpu.VMEM((2, ff, EARLY * CHUNK), BF16),
             pltpu.VMEM((2, nd, FEW, d_model), BF16),
             pltpu.VMEM((2, nd, SLOT, d_model), BF16),
-            dma((depth, 2, 2)), dma((2,)),
+            dma((depth, 2, 2)), dma((2,)), dma((2,)),
         ],
-        compiler_params=pltpu.CompilerParams(vmem_limit_bytes=36_000_000),
+        compiler_params=pltpu.CompilerParams(vmem_limit_bytes=33_800_000),
         name="routed_hidden",
-    )(cnt, xg, w1, w3, pltpu.with_memory_space_constraint(pre1, pltpu.VMEM),
+    )(cnt, xg, w1, w3, w2, pltpu.with_memory_space_constraint(pre1, pltpu.VMEM),
       pltpu.with_memory_space_constraint(pre3, pltpu.VMEM))
 
 
@@ -406,7 +427,8 @@
                 gv, wb, sdb, ob, snd, kept, in0, in1, in2,
                 gsem, wsem, dsem, s0s, s0r, s1s, s1r, s2s, s2r):
     me, core, sib, xn, yn, dg = neighbours()
-    n_exp, full, ff = hv.shape
+    n_exp, full, _ = hv.shape
+    ff = w2_hbm.shape[1]
     nd = gv.shape[0]
     rows = gv.shape[1] // 3
     n_chunks = snd.shape[0]
@@ -428,10 +450,9 @@
         return pltpu.make_async_copy(sd_hbm.at[:, cols], sdb.at[c], dsem.at[c])
 
     gcopy = pltpu.make_async_copy(g_hbm, gv, gsem)
-    for e in range(n_exp):
-        wcopy(0, e).start()
+    early = (hv.shape[2] - ff) // width
     gcopy.start()
-    for c in range(1, depth):
+    for c in range(early, early + depth):
         for e in range(n_exp):
             wcopy(c, e).start()
 
@@ -472,12 +493,11 @@
         send2(c, 1).start()
 
     def expert(c, e):
-        out = jnp.dot(hv[e], wb[c % depth, e], preferred_element_type=F32)
+        out = jnp.dot(hv[e, :, 0:ff], wb[c % depth, e], preferred_element_type=F32)
         out = out.astype(BF16).astype(F32)
         ob[:, e] = out.reshape(nd, SLOT, width)
 
-    def gated(d):
-        o = ob[d].reshape(n_exp * SLOT, width).astype(BF16)
+    def gated(d, o):
         r = jnp.dot(gv[d], o, preferred_element_type=F32)
         return r[0:rows] + r[rows:2 * rows] + r[2 * rows:3 * rows]
 
@@ -511,26 +531,35 @@
                     start2(c - 3)
 
         dcopy(c).start()
-
-        @pl.when(c == 0)
-        def _():
-            gcopy.wait()
+        reduce_start(c, lambda d: ob[d].reshape(n_exp * SLOT, width).astype(BF16))
+        return carry
+
+    def reduce_start(c, rows_of):
         chips = (own_c, xn_c, yn_c, dg_c)
         where = ((0, 0), (2, 1), (1, 2), (3, 3))
         for chip, (p0, p1) in zip(chips, where):
-            r = gated(2 * chip + 1 - core)
+            d = 2 * chip + 1 - core
+            r = gated(d, rows_of(d))
             snd[c, 0, p0] = r[:, 0:hw]
             snd[c, 1, p1] = r[:, hw:width]
         for chip, (p0, p1) in zip(chips, where):
-            r = gated(2 * chip + core)
+            d = 2 * chip + core
+            r = gated(d, rows_of(d))
             kept[c, 0, p0] = r[:, 0:hw]
             kept[c, 1, p1] = r[:, hw:width]
 
         send0(c).start()
-        return carry
 
     pl.semaphore_wait(barrier, 3)
-    lax.fori_loop(0, n_chunks, chunk, 0)
+    gcopy.wait()
+    for c in range(early):
+        dcopy(c).start()
+        cols = slice(ff + c * width, ff + (c + 1) * width)
+        reduce_start(c, lambda d: hv[:, pl.ds(pl.multiple_of(d * SLOT, SLOT), SLOT), cols].reshape(n_exp * SLOT, width))
+    for c in range(early - 1):
+        step0(c)
+        start1(c)
+    lax.fori_loop(early, n_chunks, chunk, 0)
 
     def shared(c):
         dcopy(c).wait()
@@ -577,11 +606,12 @@
 
 
 def down_call(h, g, hsh, w2, sd):
-    n_exp, full, ff = h.shape
+    n_exp, full, _ = h.shape
+    ff = w2.shape[1]
     nd, rows3, width_g = g.shape
     rows = rows3 // 3
     d_model = w2.shape[2]
-    width = 256
+    width = CHUNK
     n_chunks = d_model // width
     depth = 3
     hw = width // 2
@@ -608,7 +638,7 @@
             dma((n_chunks, 2)), dma((n_chunks, 2)), dma((n_chunks, 2)), dma((n_chunks, 2)),
         ],
         compiler_params=pltpu.CompilerParams(
-            collective_id=1, has_side_effects=True, vmem_limit_bytes=VMEM_LIMIT - H_BYTES),
+            collective_id=1, has_side_effects=True, vmem_limit_bytes=55_000_000),
         name="down_reduce",
     )(pltpu.with_memory_space_constraint(h, pltpu.VMEM), g, hsh, w2, sd)
 
@@ -618,7 +648,7 @@
 
     def device_fn(x, route, gates, w_gate, w_up, w_down, sg, su, sd):
         xg, hsh, cnt, g, pre1, pre3 = gather_call(x, route.T, gates.T, sg, su, w_gate, w_up, nd)
-        h = hidden_call(cnt, xg, w_gate, w_up, pre1, pre3)
+        h = hidden_call(cnt, xg, w_gate, w_up, w_down, pre1, pre3)
         return down_call(h.reshape(h.shape[0], -1, h.shape[3]), g, hsh, w_down, sd)
 
     tok = P(("dp", "ep"), None)

time: 108 us -> 109 us (level)
    pallas_call x1, Pallas kernels: 30.5 us -> 34 us  [hidden_call(): pl.pallas_call(hidden_kernel, out_shape=pltpu.VMEM((n_exp, nd, SLOT, ff +...]
    pallas_call x1, Pallas kernels: 48.5 us -> 45.5 us  [down_call(): pl.pallas_call(down_kernel, out_shape=jax.ShapeDtypeStruct((rows, d_model...]
where the time goes in v1:
time: 109 us
  Pallas kernels  107 us (98%)
  local copies, waits for them, and re-layouts  1.77 us (2%)
    pallas_call x1, Pallas kernels, down_call(): pl.pallas_call(down_kernel, out_shape=jax.ShapeDtypeStruct((rows, d_model...  45.5 us
    pallas_call x1, Pallas kernels, hidden_call(): pl.pallas_call(hidden_kernel, out_shape=pltpu.VMEM((n_exp, nd, SLOT, ff +...  34 us
    pallas_call x1, Pallas kernels, gather_call(): pl.pallas_call(gather_kernel, out_shape=(jax.ShapeDtypeStruct((8, nd, SLO...  27.7 us

profile of v1, /device:TPU:0, one launch (start us, length us, event | category | flops | bytes accessed | tf_op | source)
XLA Modules:
  0.0 109.0 jit_solution(16293626399558209555)
XLA Ops:
  0.0 27.7 %gather_shared.1 = (bf16[8,8,40,2048]{3,2,1,0:T(8,128)(2,1)}, bf16[96,2816]{1,0:T(8,128)(2,1)}, s32[8,8,128]{2,1,0:T(8,128)}, bf16[8,288,320]{2,1,0:T(8,128)(2,1...) custom-call(bf16[96,2048]{1,0:T(8,128)(2,1)} %x_ref.1, s32[6,96]{1,0:T(8,128)} %bitcast.4, ...), custom_call_target="tpu_custom_call" | custom-call | tf_op jit(solution)/shard_map/gather_shared/pallas_call | solution.py:249
  27.7 34.0 %routed_hidden.1 = bf16[8,8,40,1920]{3,2,1,0:T(8,128)(2,1)S(1)} custom-call(s32[8,8,128]{2,1,0:T(8,128)} %get-tuple-element.11.cnt, bf16[8,8,40,2048]{3,2,1,0:T(8,128)(2,1)} %get-tuple-element.12.xg_hbm, bf16[8,2048,1408]{2,1,0:T(8,128)(2,1)} %w1_hbm.3, bf16[8,2048,1408]{2,1,0:T(8,128)(2,1)} %w3_hbm.3, bf16[8,1408,2048]{2,1,0:T(8,128)(2,1)} %w2_hbm.3, ...), custom_call_target="tpu_custom_call" | custom-call | tf_op jit(solution)/shard_map/routed_hidden/pallas_call | solution.py:407
  61.7 45.5 %down_reduce.1 = bf16[96,2048]{1,0:T(8,128)(2,1)} custom-call(bf16[8,320,1920]{2,1,0:T(8,128)(2,1)S(1)} %bitcast.3, bf16[8,288,320]{2,1,0:T(8,128)(2,1)} %get-tuple-element.15.g_hbm, bf16[96,2816]{1,0:T(8,128)(2,1)} %get-tuple-element.16.hsh_ref, bf16[8,1408,2048]{2,1,0:T(8,128)(2,1)} %w2_hbm.3, bf16[2816,2048]{1,0:T(8,128)(2,1)} %sd_hbm.1), custom_call_target="tpu_custom_call" | custom-call | tf_op jit(solution)/shard_map/down_reduce/pallas_call | solution.py:621
  107.2 1.8 %copy.11 = bf16[96,2048]{1,0:T(8,128)(2,1)} copy(bf16[96,2048]{1,0:T(8,128)(2,1)} %down_reduce.1) | data formatting | bytes 786432

commit v2 on v1

--- a/solution.py
+++ b/solution.py
@@ -131,10 +131,8 @@
             return carry
         lax.fori_loop(lo, hi, body, 0)
 
-    shared_range(0, 2)
+    shared_range(0, n_chunks - 6)
     prefetch(0)
-    shared_range(2, n_chunks - 5)
-    prefetch(1)
 
     for c in metas:
         c.wait_recv()
@@ -175,11 +173,34 @@
     sy1 = rcopy(land.at[yn, hs(1)], land.at[yn, hs(1)], ss_s.at[2], ss_r.at[2], sib)
     sy1.start()
 
-    shared_range(n_chunks - 5, n_chunks)
-    for e in range(2, pre1.shape[0]):
+    shared_range(n_chunks - 6, n_chunks)
+    for e in range(1, pre1.shape[0]):
         prefetch(e)
     hcopy = pltpu.make_async_copy(hsh, hsh_hbm, hsem)
     hcopy.start()
+
+    width_g = 8 * SLOT
+    lane = lax.broadcasted_iota(jnp.int32, (8, width_g), 1)
+    sel = jnp.where(lane // SLOT == lax.broadcasted_iota(jnp.int32, (8, width_g), 0), 1.0, 0.0)
+    slot_id = (lax.broadcasted_iota(jnp.int32, (rows, width_g), 1) % SLOT).astype(F32)
+
+    def spread(v):
+        return lax.dot_general(v, sel, (((0,), (0,)), ((), ())), preferred_element_type=F32)[:rows]
+
+    def gate_body(d, carry):
+        rk = metal[d, 0:8, :]
+        gt = metal[d, 8:16, :]
+        hi = gt.astype(BF16).astype(F32)
+        mid = (gt - hi).astype(BF16).astype(F32)
+        lo = gt - hi - mid
+        eq = spread(rk) == slot_id
+        for q, part in enumerate((hi, mid, lo)):
+            gv[d, q * rows:(q + 1) * rows, :] = jnp.where(eq, spread(part), 0.0).astype(BF16)
+        return carry
+
+    lax.fori_loop(0, nd, gate_body, 0)
+    gcopy = pltpu.make_async_copy(gv, g_hbm, gsem)
+    gcopy.start()
 
     own_x[1].wait_recv()
     sx1 = rcopy(land.at[xn, hs(1)], land.at[xn, hs(1)], ss_s.at[3], ss_r.at[3], sib)
@@ -195,29 +216,6 @@
     sy1.wait_recv()
     sy0.wait_recv()
     pick(syn, land.at[syn], 5)
-
-    width_g = 8 * SLOT
-    lane = lax.broadcasted_iota(jnp.int32, (8, width_g), 1)
-    sel = jnp.where(lane // SLOT == lax.broadcasted_iota(jnp.int32, (8, width_g), 0), 1.0, 0.0)
-    slot_id = (lax.broadcasted_iota(jnp.int32, (rows, width_g), 1) % SLOT).astype(F32)
-
-    def spread(v):
-        return lax.dot_general(v, sel, (((0,), (0,)), ((), ())), preferred_element_type=F32)[:rows]
-
-    def gate_body(d, carry):
-        rk = metal[d, 0:8, :]
-        gt = metal[d, 8:16, :]
-        hi = gt.astype(BF16).astype(F32)
-        mid = (gt - hi).astype(BF16).astype(F32)
-        lo = gt - hi - mid
-        eq = spread(rk) == slot_id
-        for q, part in enumerate((hi, mid, lo)):
-            gv[d, q * rows:(q + 1) * rows, :] = jnp.where(eq, spread(part), 0.0).astype(BF16)
-        return carry
-
-    lax.fori_loop(0, nd, gate_body, 0)
-    gcopy = pltpu.make_async_copy(gv, g_hbm, gsem)
-    gcopy.start()
 
     fy.wait_recv()
     sd0 = rcopy(land.at[dg, hs(0)], land.at[dg, hs(0)], ss_s.at[5], ss_r.at[5], sib)
@@ -242,7 +240,7 @@
     rows, d_model = x.shape
     ff = sg.shape[1]
     width = 256
-    ring = 4
+    ring = 8
     any_spec = pl.BlockSpec(memory_space=pl.ANY)
     vmem = pl.BlockSpec(memory_space=pltpu.VMEM)
     dma = pltpu.SemaphoreType.DMA
@@ -345,7 +343,7 @@
             out = jnp.dot(rows, wb2[e % 2, :, c0:c0 + 256], preferred_element_type=F32)
             h_ref[e, :, 0:slots, ff + c0:ff + c0 + 256] = out.astype(BF16).reshape(nd, slots, 256)
 
-    def expert(e, gate, up, wait):
+    def expert(e, gate, up, wait, refill):
         small = few(e)
 
         @pl.when(small)
@@ -355,6 +353,7 @@
                 wait(j)
                 for c0, w in cols:
                     h_ref[e, :, 0:FEW, c0:c0 + w] = hidden(xfew.at[e % 2], up, gate, c0, w)
+                refill(j)
             dcopy(e).wait()
             down(e, FEW)
 
@@ -365,6 +364,7 @@
                 wait(j)
                 for c0, w in cols:
                     h_ref[e, :, :, c0:c0 + w] = hidden(xall.at[e % 2], up, gate, c0, w)
+                refill(j)
             dcopy(e).wait()
             down(e, SLOT)
 
@@ -374,7 +374,7 @@
             dcopy(e + 2).start()
 
     def early(e, carry):
-        expert(e, pre1.at[e], pre3.at[e], lambda j: None)
+        expert(e, pre1.at[e], pre3.at[e], lambda j: None, lambda j: None)
         return carry
 
     def late(e, carry):
@@ -384,13 +384,13 @@
             for c in wcopy(e, slot, j):
                 c.wait()
 
-        expert(e, wb1.at[slot], wb3.at[slot], wait)
-
-        @pl.when(e + depth < n_exp)
-        def _():
-            for j in range(len(groups)):
+        def refill(j):
+            @pl.when(e + depth < n_exp)
+            def _():
                 for c in wcopy(e + depth, slot, j):
                     c.start()
+
+        expert(e, wb1.at[slot], wb3.at[slot], wait, refill)
         return carry
 
     lax.fori_loop(0, first, early, 0)
@@ -514,24 +514,19 @@
                     wcopy(c + depth, e).start()
 
             if e0 == 0:
-                @pl.when(c >= 1)
+                step0(c - 1)
+                start1(c - 1)
+
+                @pl.when(c == early)
                 def _():
-                    step0(c - 1)
-
-                @pl.when(c >= 3)
-                def _():
-                    step1(c - 3)
-
-                @pl.when(c >= 1)
-                def _():
-                    start1(c - 1)
-
-                @pl.when(c >= 3)
-                def _():
-                    start2(c - 3)
+                    for i in range(early - 2):
+                        step1(i)
+                        start2(i)
 
         dcopy(c).start()
         reduce_start(c, lambda d: ob[d].reshape(n_exp * SLOT, width).astype(BF16))
+        step1(c - 2)
+        start2(c - 2)
         return carry
 
     def reduce_start(c, rows_of):
@@ -573,27 +568,26 @@
             return carry
         lax.fori_loop(lo, hi, body, 0)
 
+    def finish_range(lo, hi):
+        def body(c, carry):
+            step2(c)
+            for q in range(2):
+                cols = pl.ds(pl.multiple_of(c * width + q * hw, hw), hw)
+                y_ref[:, cols] = (y_ref[:, cols].astype(F32) + kept[c, q, 0]).astype(BF16)
+            return carry
+        lax.fori_loop(lo, hi, body, 0)
+
     last = n_chunks - 1
     shared_range(0, 3)
     step0(last)
-    step1(last - 2)
     start1(last)
-    start2(last - 2)
-    shared_range(3, 6)
+    shared_range(3, n_chunks)
     step1(last - 1)
     start2(last - 1)
-    shared_range(6, n_chunks)
+    finish_range(0, last - 1)
     step1(last)
     start2(last)
-
-    def finish(c, carry):
-        step2(c)
-        for q in range(2):
-            cols = pl.ds(pl.multiple_of(c * width + q * hw, hw), hw)
-            y_ref[:, cols] = (y_ref[:, cols].astype(F32) + kept[c, q, 0]).astype(BF16)
-        return carry
-
-    lax.fori_loop(0, n_chunks, finish, 0)
+    finish_range(last - 1, n_chunks)
 
     def drain(c, carry):
         send0(c).wait_send()

time: 109 us -> 105 us (0.963)
  Pallas kernels: 107 us -> 103 us
    pallas_call x1, Pallas kernels: 27.7 us -> 23.8 us  [gather_call(): pl.pallas_call(gather_kernel, out_shape=(jax.ShapeDtypeStruct((8, nd, SLO...]
where the time goes in v2:
time: 105 us
  Pallas kernels  103 us (98%)
  local copies, waits for them, and re-layouts  1.77 us (2%)
    pallas_call x1, Pallas kernels, down_call(): pl.pallas_call(down_kernel, out_shape=jax.ShapeDtypeStruct((rows, d_model...  44.8 us
    pallas_call x1, Pallas kernels, hidden_call(): pl.pallas_call(hidden_kernel, out_shape=pltpu.VMEM((n_exp, nd, SLOT, ff +...  34.5 us
    pallas_call x1, Pallas kernels, gather_call(): pl.pallas_call(gather_kernel, out_shape=(jax.ShapeDtypeStruct((8, nd, SLO...  23.8 us

profile of v2, /device:TPU:0, one launch (start us, length us, event | category | flops | bytes accessed | tf_op | source)
XLA Modules:
  0.0 104.8 jit_solution(495980588055913752)
XLA Ops:
  0.0 23.8 %gather_shared.1 = (bf16[8,8,40,2048]{3,2,1,0:T(8,128)(2,1)}, bf16[96,2816]{1,0:T(8,128)(2,1)}, s32[8,8,128]{2,1,0:T(8,128)}, bf16[8,288,320]{2,1,0:T(8,128)(2,1...) custom-call(bf16[96,2048]{1,0:T(8,128)(2,1)} %x_ref.1, s32[6,96]{1,0:T(8,128)} %bitcast.4, ...), custom_call_target="tpu_custom_call" | custom-call | tf_op jit(solution)/shard_map/gather_shared/pallas_call | solution.py:247
  23.8 34.5 %routed_hidden.1 = bf16[8,8,40,1920]{3,2,1,0:T(8,128)(2,1)S(1)} custom-call(s32[8,8,128]{2,1,0:T(8,128)} %get-tuple-element.11.cnt, bf16[8,8,40,2048]{3,2,1,0:T(8,128)(2,1)} %get-tuple-element.12.xg_hbm, bf16[8,2048,1408]{2,1,0:T(8,128)(2,1)} %w1_hbm.3, bf16[8,2048,1408]{2,1,0:T(8,128)(2,1)} %w3_hbm.3, bf16[8,1408,2048]{2,1,0:T(8,128)(2,1)} %w2_hbm.3, ...), custom_call_target="tpu_custom_call" | custom-call | tf_op jit(solution)/shard_map/routed_hidden/pallas_call | solution.py:407
  58.3 44.8 %down_reduce.1 = bf16[96,2048]{1,0:T(8,128)(2,1)} custom-call(bf16[8,320,1920]{2,1,0:T(8,128)(2,1)S(1)} %bitcast.3, bf16[8,288,320]{2,1,0:T(8,128)(2,1)} %get-tuple-element.15.g_hbm, bf16[96,2816]{1,0:T(8,128)(2,1)} %get-tuple-element.16.hsh_ref, bf16[8,1408,2048]{2,1,0:T(8,128)(2,1)} %w2_hbm.3, bf16[2816,2048]{1,0:T(8,128)(2,1)} %sd_hbm.1), custom_call_target="tpu_custom_call" | custom-call | tf_op jit(solution)/shard_map/down_reduce/pallas_call | solution.py:615
  103.1 1.8 %copy.11 = bf16[96,2048]{1,0:T(8,128)(2,1)} copy(bf16[96,2048]{1,0:T(8,128)(2,1)} %down_reduce.1) | data formatting | bytes 786432

commit v3 on v2

--- a/solution.py
+++ b/solution.py
@@ -13,6 +13,7 @@
 VMEM_LIMIT = 67_000_000
 H_BYTES = 10_500_000
 CHUNK = 256
+GROUP = 8
 EARLY = 2
 PRE = 2
 PRE_BYTES = 23_500_000
@@ -452,9 +453,8 @@
     gcopy = pltpu.make_async_copy(g_hbm, gv, gsem)
     early = (hv.shape[2] - ff) // width
     gcopy.start()
-    for c in range(early, early + depth):
-        for e in range(n_exp):
-            wcopy(c, e).start()
+    for e in range(n_exp):
+        wcopy(early, e).start()
 
     own_c, xn_c, yn_c, dg_c = me // 2, xn // 2, yn // 2, dg // 2
     orders = ((own_c, yn_c, xn_c, dg_c), (own_c, xn_c, yn_c, dg_c))
@@ -502,15 +502,15 @@
         return r[0:rows] + r[rows:2 * rows] + r[2 * rows:3 * rows]
 
     def chunk(c, carry):
-        for e0 in range(0, n_exp, 4):
-            for e in range(e0, e0 + 4):
+        for e0 in range(0, n_exp, GROUP):
+            for e in range(e0, e0 + GROUP):
                 wcopy(c, e).wait()
-            for e in range(e0, e0 + 4):
+            for e in range(e0, e0 + GROUP):
                 expert(c, e)
 
             @pl.when(c + depth < n_chunks)
             def _():
-                for e in range(e0, e0 + 4):
+                for e in range(e0, e0 + GROUP):
                     wcopy(c + depth, e).start()
 
             if e0 == 0:
@@ -548,9 +548,13 @@
     pl.semaphore_wait(barrier, 3)
     gcopy.wait()
     for c in range(early):
-        dcopy(c).start()
         cols = slice(ff + c * width, ff + (c + 1) * width)
         reduce_start(c, lambda d: hv[:, pl.ds(pl.multiple_of(d * SLOT, SLOT), SLOT), cols].reshape(n_exp * SLOT, width))
+    for c in range(early + 1, early + depth):
+        for e in range(n_exp):
+            wcopy(c, e).start()
+    for c in range(early):
+        dcopy(c).start()
     for c in range(early - 1):
         step0(c)
         start1(c)

time: 105 us -> 101 us (0.962)
  Pallas kernels: 103 us -> 98.2 us
    pallas_call x1, Pallas kernels: 44.8 us -> 38.2 us  [down_call(): pl.pallas_call(down_kernel, out_shape=jax.ShapeDtypeStruct((rows, d_model...]
    pallas_call x1, Pallas kernels: 34.5 us -> 36.3 us  [hidden_call(): pl.pallas_call(hidden_kernel, out_shape=pltpu.VMEM((n_exp, nd, SLOT, ff +...]
where the time goes in v3:
time: 101 us; the launch traced here: 100 us
  Pallas kernels  98.2 us (97%)
  local copies, waits for them, and re-layouts  1.77 us (2%)
    pallas_call x1, Pallas kernels, down_call(): pl.pallas_call(down_kernel, out_shape=jax.ShapeDtypeStruct((rows, d_model...  38.2 us
    pallas_call x1, Pallas kernels, hidden_call(): pl.pallas_call(hidden_kernel, out_shape=pltpu.VMEM((n_exp, nd, SLOT, ff +...  36.3 us
    pallas_call x1, Pallas kernels, gather_call(): pl.pallas_call(gather_kernel, out_shape=(jax.ShapeDtypeStruct((8, nd, SLO...  23.8 us

profile of v3, /device:TPU:0, one launch (start us, length us, event | category | flops | bytes accessed | tf_op | source)
XLA Modules:
  0.0 100.0 jit_solution(17570574820589788900)
XLA Ops:
  0.0 23.8 %gather_shared.1 = (bf16[8,8,40,2048]{3,2,1,0:T(8,128)(2,1)}, bf16[96,2816]{1,0:T(8,128)(2,1)}, s32[8,8,128]{2,1,0:T(8,128)}, bf16[8,288,320]{2,1,0:T(8,128)(2,1...) custom-call(bf16[96,2048]{1,0:T(8,128)(2,1)} %x_ref.1, s32[6,96]{1,0:T(8,128)} %bitcast.4, ...), custom_call_target="tpu_custom_call" | custom-call | tf_op jit(solution)/shard_map/gather_shared/pallas_call | solution.py:248
  23.8 36.3 %routed_hidden.1 = bf16[8,8,40,1920]{3,2,1,0:T(8,128)(2,1)S(1)} custom-call(s32[8,8,128]{2,1,0:T(8,128)} %get-tuple-element.11.cnt, bf16[8,8,40,2048]{3,2,1,0:T(8,128)(2,1)} %get-tuple-element.12.xg_hbm, bf16[8,2048,1408]{2,1,0:T(8,128)(2,1)} %w1_hbm.3, bf16[8,2048,1408]{2,1,0:T(8,128)(2,1)} %w3_hbm.3, bf16[8,1408,2048]{2,1,0:T(8,128)(2,1)} %w2_hbm.3, ...), custom_call_target="tpu_custom_call" | custom-call | tf_op jit(solution)/shard_map/routed_hidden/pallas_call | solution.py:408
  60.1 38.2 %down_reduce.1 = bf16[96,2048]{1,0:T(8,128)(2,1)} custom-call(bf16[8,320,1920]{2,1,0:T(8,128)(2,1)S(1)} %bitcast.3, bf16[8,288,320]{2,1,0:T(8,128)(2,1)} %get-tuple-element.15.g_hbm, bf16[96,2816]{1,0:T(8,128)(2,1)} %get-tuple-element.16.hsh_ref, bf16[8,1408,2048]{2,1,0:T(8,128)(2,1)} %w2_hbm.3, bf16[2816,2048]{1,0:T(8,128)(2,1)} %sd_hbm.1), custom_call_target="tpu_custom_call" | custom-call | tf_op jit(solution)/shard_map/down_reduce/pallas_call | solution.py:619
  98.3 1.8 %copy.11 = bf16[96,2048]{1,0:T(8,128)(2,1)} copy(bf16[96,2048]{1,0:T(8,128)(2,1)} %down_reduce.1) | data formatting | bytes 786432

commit v4 on v3

--- a/solution.py
+++ b/solution.py
@@ -14,7 +14,7 @@
 H_BYTES = 10_500_000
 CHUNK = 256
 GROUP = 8
-EARLY = 2
+EARLY = 1
 PRE = 2
 PRE_BYTES = 23_500_000
 BF16 = jnp.bfloat16
@@ -39,10 +39,10 @@
         device_id={"ep": dev}, device_id_type=MESH)
 
 
-def gather_kernel(x_ref, route_ref, gate_ref, sg_hbm, su_hbm, w1_hbm, w3_hbm,
+def gather_kernel(x_hbm, route_hbm, gate_hbm, sg_hbm, su_hbm, w1_hbm, w3_hbm,
                   xg_hbm, hsh_hbm, cnt_hbm, g_hbm, pre1, pre3,
-                  land, meta_s, bg, bu, metal, stage, hsh, gv, cntv,
-                  wsem, osem, psem, gsem, hsem, csem,
+                  x_ref, route_ref, gate_ref, land, meta_s, bg, bu, metal, stage, hsh, gv, cntv,
+                  isem, wsem, osem, psem, gsem, hsem, csem,
                   sx_s, sx_r, sy_s, sy_r, f_s, f_r, ss_s, ss_r, m_s, m_r):
     me, core, sib, xn, yn, dg = neighbours()
     sxn = xn + 1 - 2 * core
@@ -56,6 +56,10 @@
     n_chunks = sg_hbm.shape[1] // width
     n_all = 8 * nd
 
+    ins = [pltpu.make_async_copy(src, dst, isem.at[i]) for i, (src, dst) in enumerate(
+        ((route_hbm, route_ref), (gate_hbm, gate_ref), (x_hbm, x_ref)))]
+    for c in ins:
+        c.start()
     barrier = pltpu.get_barrier_semaphore()
     for r in range(1, nd):
         pl.semaphore_signal(barrier, inc=1, device_id={"ep": (me + r) % nd}, device_id_type=MESH)
@@ -78,6 +82,8 @@
         for c in pcopy(e):
             c.start()
 
+    ins[0].wait()
+    ins[1].wait()
     ids = lax.broadcasted_iota(jnp.int32, (n_all, rows), 0)
     mask = jnp.zeros((n_all, rows), F32)
     gmap = jnp.zeros((n_all, rows), F32)
@@ -107,6 +113,7 @@
         c = rcopy(meta_s.at[dst], metal.at[me], m_s.at[r - 1], m_r.at[r - 1], dst)
         c.start()
         metas.append(c)
+    ins[2].wait()
     own_x = [rcopy(x_ref.at[hs(h)], land.at[me, hs(h)], sx_s.at[h], sx_r.at[h], xn) for h in range(2)]
     own_y = [rcopy(x_ref.at[hs(h)], land.at[me, hs(h)], sy_s.at[h], sy_r.at[h], yn) for h in range(2)]
     own_s = rcopy(x_ref, land.at[me], ss_s.at[0], ss_r.at[0], sib)
@@ -255,9 +262,12 @@
             pltpu.VMEM((PRE,) + w1.shape[1:], BF16),
             pltpu.VMEM((PRE,) + w3.shape[1:], BF16),
         ),
-        in_specs=[vmem, vmem, vmem] + [any_spec] * 4,
+        in_specs=[any_spec] * 7,
         out_specs=(pl.BlockSpec(memory_space=pltpu.HBM),) * 4 + (vmem, vmem),
         scratch_shapes=[
+            pltpu.VMEM(x.shape, BF16),
+            pltpu.VMEM(route.shape, jnp.int32),
+            pltpu.VMEM(gates.shape, F32),
             pltpu.VMEM((nd, rows, d_model), BF16),
             pltpu.VMEM((nd, 16, 128), F32),
             pltpu.VMEM((ring, d_model, width), BF16),
@@ -267,7 +277,7 @@
             pltpu.VMEM((rows, ff), BF16),
             pltpu.VMEM((nd, 3 * rows, 8 * SLOT), BF16),
             pltpu.VMEM((nd, 8, 128), jnp.int32),
-            dma((2, ring)),
+            dma((3,)), dma((2, ring)),
             dma((8,)), dma((2, PRE)), dma(()), dma(()), dma(()),
             dma((2,)), dma((2,)), dma((2,)), dma((2,)), dma((2,)), dma((2,)),
             dma((7,)), dma((7,)), dma((7,)), dma((7,)),
@@ -281,8 +291,8 @@
 FEW = 16
 
 
-def hidden_kernel(cnt, xg_hbm, w1_hbm, w3_hbm, w2_hbm, pre1, pre3, h_ref,
-                  wb1, wb3, wb2, xfew, xall, wsem, dsem, xsem):
+def hidden_kernel(cnt_hbm, xg_hbm, w1_hbm, w3_hbm, w2_hbm, pre1, pre3, h_ref,
+                  cnt, wb1, wb3, wb2, xfew, xall, csem, wsem, dsem, xsem):
     n_exp, d_model, ff = w1_hbm.shape
     nd = cnt.shape[0]
     depth = wb1.shape[0]
@@ -322,15 +332,19 @@
     def dcopy(e):
         return pltpu.make_async_copy(w2_hbm.at[e, :, pl.ds(0, early_w)], wb2.at[e % 2], dsem.at[e % 2])
 
-    rows_start(0)
+    ccopy = pltpu.make_async_copy(cnt_hbm, cnt, csem)
+    ccopy.start()
     dcopy(0).start()
-    rows_start(1)
     dcopy(1).start()
     for e in range(first, first + depth):
         for j in range(len(groups)):
             for c in wcopy(e, e % depth, j):
                 c.start()
-    h_ref[...] = jnp.zeros_like(h_ref)
+    ccopy.wait()
+    rows_start(0)
+    rows_start(1)
+    for e in range(n_exp):
+        h_ref[e, :, FEW:SLOT, :] = jnp.zeros((nd, SLOT - FEW, h_ref.shape[3]), BF16)
 
     def hidden(rows_ref, up, gate, c0, w):
         m = rows_ref.shape[0] * rows_ref.shape[1]
@@ -408,15 +422,16 @@
     return pl.pallas_call(
         hidden_kernel,
         out_shape=pltpu.VMEM((n_exp, nd, SLOT, ff + EARLY * CHUNK), BF16),
-        in_specs=[pl.BlockSpec(memory_space=pltpu.SMEM)] + [any_spec] * 4 + [vmem, vmem],
+        in_specs=[any_spec] * 5 + [vmem, vmem],
         out_specs=vmem,
         scratch_shapes=[
+            pltpu.SMEM(cnt.shape, jnp.int32),
             pltpu.VMEM((depth, d_model, ff), BF16),
             pltpu.VMEM((depth, d_model, ff), BF16),
             pltpu.VMEM((2, ff, EARLY * CHUNK), BF16),
             pltpu.VMEM((2, nd, FEW, d_model), BF16),
             pltpu.VMEM((2, nd, SLOT, d_model), BF16),
-            dma((depth, 2, 2)), dma((2,)), dma((2,)),
+            dma(()), dma((depth, 2, 2)), dma((2,)), dma((2,)),
         ],
         compiler_params=pltpu.CompilerParams(vmem_limit_bytes=33_800_000),
         name="routed_hidden",
@@ -424,9 +439,9 @@
       pltpu.with_memory_space_constraint(pre3, pltpu.VMEM))
 
 
-def down_kernel(hv, g_hbm, hsh_ref, w2_hbm, sd_hbm, y_ref,
-                gv, wb, sdb, ob, snd, kept, in0, in1, in2,
-                gsem, wsem, dsem, s0s, s0r, s1s, s1r, s2s, s2r):
+def down_kernel(hv, g_hbm, hsh_hbm, w2_hbm, sd_hbm, y_hbm,
+                hsh_ref, y_ref, gv, wb, sdb, ob, snd, kept, in0, in1, in2,
+                isem, ysem, gsem, wsem, dsem, s0s, s0r, s1s, s1r, s2s, s2r):
     me, core, sib, xn, yn, dg = neighbours()
     n_exp, full, _ = hv.shape
     ff = w2_hbm.shape[1]
@@ -455,6 +470,8 @@
     gcopy.start()
     for e in range(n_exp):
         wcopy(early, e).start()
+    scopy = pltpu.make_async_copy(hsh_hbm, hsh_ref, isem)
+    scopy.start()
 
     own_c, xn_c, yn_c, dg_c = me // 2, xn // 2, yn // 2, dg // 2
     orders = ((own_c, yn_c, xn_c, dg_c), (own_c, xn_c, yn_c, dg_c))
@@ -525,8 +542,11 @@
 
         dcopy(c).start()
         reduce_start(c, lambda d: ob[d].reshape(n_exp * SLOT, width).astype(BF16))
-        step1(c - 2)
-        start2(c - 2)
+
+        @pl.when(c >= 2)
+        def _():
+            step1(c - 2)
+            start2(c - 2)
         return carry
 
     def reduce_start(c, rows_of):
@@ -582,6 +602,7 @@
         lax.fori_loop(lo, hi, body, 0)
 
     last = n_chunks - 1
+    scopy.wait()
     shared_range(0, 3)
     step0(last)
     start1(last)
@@ -589,9 +610,14 @@
     step1(last - 1)
     start2(last - 1)
     finish_range(0, last - 1)
+    cut = (last - 1) * width
+    ycopies = [pltpu.make_async_copy(y_ref.at[:, a:b], y_hbm.at[:, a:b], ysem.at[i])
+               for i, (a, b) in enumerate(((0, cut), (cut, n_chunks * width)))]
+    ycopies[0].start()
     step1(last)
     start2(last)
     finish_range(last - 1, n_chunks)
+    ycopies[1].start()
 
     def drain(c, carry):
         send0(c).wait_send()
@@ -601,6 +627,8 @@
         return carry
 
     lax.fori_loop(0, n_chunks, drain, 0)
+    for c in ycopies:
+        c.wait()
 
 
 def down_call(h, g, hsh, w2, sd):
@@ -619,9 +647,11 @@
     return pl.pallas_call(
         down_kernel,
         out_shape=jax.ShapeDtypeStruct((rows, d_model), BF16),
-        in_specs=[vmem, any_spec, vmem, any_spec, any_spec],
-        out_specs=vmem,
+        in_specs=[vmem] + [any_spec] * 4,
+        out_specs=pl.BlockSpec(memory_space=pltpu.HBM),
         scratch_shapes=[
+            pltpu.VMEM(hsh.shape, BF16),
+            pltpu.VMEM((rows, d_model), BF16),
             pltpu.VMEM((nd, rows3, width_g), BF16),
             pltpu.VMEM((depth, n_exp, ff, width), BF16),
             pltpu.VMEM((n_chunks, sd.shape[0], width), BF16),
@@ -631,7 +661,7 @@
             pltpu.VMEM((n_chunks, 2, 4, rows, hw), F32),
             pltpu.VMEM((n_chunks, 2, 2, rows, hw), F32),
             pltpu.VMEM((n_chunks, 2, rows, hw), F32),
-            dma(()), dma((depth, n_exp)), dma((n_chunks,)),
+            dma(()), dma((2,)), dma(()), dma((depth, n_exp)), dma((n_chunks,)),
             dma((n_chunks,)), dma((n_chunks,)),
             dma((n_chunks, 2)), dma((n_chunks, 2)), dma((n_chunks, 2)), dma((n_chunks, 2)),
         ],

time: 101 us -> 96.9 us (0.959)
  Pallas kernels: 98.2 us -> 93.8 us
    pallas_call x1, Pallas kernels: 36.3 us -> 34.1 us  [hidden_call(): pl.pallas_call(hidden_kernel, out_shape=pltpu.VMEM((n_exp, nd, SLOT, ff +...]
    pallas_call x1, Pallas kernels: 38.2 us -> 36.8 us  [down_call(): pl.pallas_call(down_kernel, out_shape=jax.ShapeDtypeStruct((rows, d_model...]
where the time goes in v4:
time: 96.9 us; the launch traced here: 95.6 us
  Pallas kernels  93.8 us (97%)
  local copies, waits for them, and re-layouts  1.77 us (2%)
    pallas_call x1, Pallas kernels, down_call(): pl.pallas_call(down_kernel, out_shape=jax.ShapeDtypeStruct((rows, d_model...  36.8 us
    pallas_call x1, Pallas kernels, hidden_call(): pl.pallas_call(hidden_kernel, out_shape=pltpu.VMEM((n_exp, nd, SLOT, ff +...  34.1 us
    pallas_call x1, Pallas kernels, gather_call(): pl.pallas_call(gather_kernel, out_shape=(jax.ShapeDtypeStruct((8, nd, SLO...  22.8 us

profile of v4, /device:TPU:0, one launch (start us, length us, event | category | flops | bytes accessed | tf_op | source)
XLA Modules:
  0.0 95.6 jit_solution(2180440620302806751)
XLA Ops:
  0.0 22.8 %gather_shared.1 = (bf16[8,8,40,2048]{3,2,1,0:T(8,128)(2,1)}, bf16[96,2816]{1,0:T(8,128)(2,1)}, s32[8,8,128]{2,1,0:T(8,128)}, bf16[8,288,320]{2,1,0:T(8,128)(2,1...) custom-call(bf16[96,2048]{1,0:T(8,128)(2,1)} %x_hbm.1, s32[6,96]{1,0:T(8,128)} %bitcast.4, ...), custom_call_target="tpu_custom_call" | custom-call | tf_op jit(solution)/shard_map/gather_shared/pallas_call | solution.py:255
  22.8 34.1 %routed_hidden.1 = bf16[8,8,40,1664]{3,2,1,0:T(8,128)(2,1)S(1)} custom-call(s32[8,8,128]{2,1,0:T(8,128)} %get-tuple-element.11.cnt_hbm, bf16[8,8,40,2048]{3,2,1,0:T(8,128)(2,1)} %get-tuple-element.12.xg_hbm, bf16[8,2048,1408]{2,1,0:T(8,128)(2,1)} %w1_hbm.3, bf16[8,2048,1408]{2,1,0:T(8,128)(2,1)} %w3_hbm.3, bf16[8,1408,2048]{2,1,0:T(8,128)(2,1)} %w2_hbm.3, ...), custom_call_target="tpu_custom_call" | custom-call | tf_op jit(solution)/shard_map/routed_hidden/pallas_call | solution.py:422
  57.0 36.8 %down_reduce.1 = bf16[96,2048]{1,0:T(8,128)(2,1)} custom-call(bf16[8,320,1664]{2,1,0:T(8,128)(2,1)S(1)} %bitcast.3, bf16[8,288,320]{2,1,0:T(8,128)(2,1)} %get-tuple-element.15.g_hbm, bf16[96,2816]{1,0:T(8,128)(2,1)} %get-tuple-element.16.hsh_hbm, bf16[8,1408,2048]{2,1,0:T(8,128)(2,1)} %w2_hbm.3, bf16[2816,2048]{1,0:T(8,128)(2,1)} %sd_hbm.1), custom_call_target="tpu_custom_call" | custom-call | tf_op jit(solution)/shard_map/down_reduce/pallas_call | solution.py:647
  93.8 1.8 %copy.11 = bf16[96,2048]{1,0:T(8,128)(2,1)} copy(bf16[96,2048]{1,0:T(8,128)(2,1)} %down_reduce.1) | data formatting | bytes 786432

commit v5 on v4

--- a/solution.py
+++ b/solution.py
@@ -13,7 +13,7 @@
 VMEM_LIMIT = 67_000_000
 H_BYTES = 10_500_000
 CHUNK = 256
-GROUP = 8
+GROUP = 4
 EARLY = 1
 PRE = 2
 PRE_BYTES = 23_500_000
@@ -39,10 +39,10 @@
         device_id={"ep": dev}, device_id_type=MESH)
 
 
-def gather_kernel(x_hbm, route_hbm, gate_hbm, sg_hbm, su_hbm, w1_hbm, w3_hbm,
-                  xg_hbm, hsh_hbm, cnt_hbm, g_hbm, pre1, pre3,
+def gather_kernel(x_hbm, route_hbm, gate_hbm, sg_hbm, su_hbm, w1_hbm, w3_hbm, w2_hbm,
+                  xg_hbm, hsh_hbm, cnt_hbm, g_hbm, pre1, pre3, pre2,
                   x_ref, route_ref, gate_ref, land, meta_s, bg, bu, metal, stage, hsh, gv, cntv,
-                  isem, wsem, osem, psem, gsem, hsem, csem,
+                  isem, wsem, osem, psem, p2sem, gsem, hsem, csem,
                   sx_s, sx_r, sy_s, sy_r, f_s, f_r, ss_s, ss_r, m_s, m_r):
     me, core, sib, xn, yn, dg = neighbours()
     sxn = xn + 1 - 2 * core
@@ -184,6 +184,8 @@
     shared_range(n_chunks - 6, n_chunks)
     for e in range(1, pre1.shape[0]):
         prefetch(e)
+    p2copy = pltpu.make_async_copy(w2_hbm.at[:, :, pl.ds(0, pre2.shape[2])], pre2, p2sem)
+    p2copy.start()
     hcopy = pltpu.make_async_copy(hsh, hsh_hbm, hsem)
     hcopy.start()
 
@@ -237,14 +239,14 @@
     pick(sdg, land.at[sdg], 7)
     for c in own_x + own_y + [own_s, fy, fx, sx0, sx1, sy0, sy1, sd0, sd1] + metas:
         c.wait_send()
-    for c in outs[6:] + [ccopy, hcopy, gcopy]:
+    for c in outs[6:] + [ccopy, hcopy, gcopy, p2copy]:
         c.wait()
     for e in range(pre1.shape[0]):
         for c in pcopy(e):
             c.wait()
 
 
-def gather_call(x, route, gates, sg, su, w1, w3, nd):
+def gather_call(x, route, gates, sg, su, w1, w3, w2, nd):
     rows, d_model = x.shape
     ff = sg.shape[1]
     width = 256
@@ -261,9 +263,10 @@
             jax.ShapeDtypeStruct((nd, 3 * rows, 8 * SLOT), BF16),
             pltpu.VMEM((PRE,) + w1.shape[1:], BF16),
             pltpu.VMEM((PRE,) + w3.shape[1:], BF16),
+            pltpu.VMEM(w2.shape[:2] + (EARLY * CHUNK,), BF16),
         ),
-        in_specs=[any_spec] * 7,
-        out_specs=(pl.BlockSpec(memory_space=pltpu.HBM),) * 4 + (vmem, vmem),
+        in_specs=[any_spec] * 8,
+        out_specs=(pl.BlockSpec(memory_space=pltpu.HBM),) * 4 + (vmem, vmem, vmem),
         scratch_shapes=[
             pltpu.VMEM(x.shape, BF16),
             pltpu.VMEM(route.shape, jnp.int32),
@@ -278,21 +281,21 @@
             pltpu.VMEM((nd, 3 * rows, 8 * SLOT), BF16),
             pltpu.VMEM((nd, 8, 128), jnp.int32),
             dma((3,)), dma((2, ring)),
-            dma((8,)), dma((2, PRE)), dma(()), dma(()), dma(()),
+            dma((8,)), dma((2, PRE)), dma(()), dma(()), dma(()), dma(()),
             dma((2,)), dma((2,)), dma((2,)), dma((2,)), dma((2,)), dma((2,)),
             dma((7,)), dma((7,)), dma((7,)), dma((7,)),
         ],
         compiler_params=pltpu.CompilerParams(
-            collective_id=0, has_side_effects=True, vmem_limit_bytes=33_800_000),
+            collective_id=0, has_side_effects=True, vmem_limit_bytes=29_500_000),
         name="gather_shared",
-    )(x, route, gates, sg, su, w1, w3)
+    )(x, route, gates, sg, su, w1, w3, w2)
 
 
 FEW = 16
 
 
-def hidden_kernel(cnt_hbm, xg_hbm, w1_hbm, w3_hbm, w2_hbm, pre1, pre3, h_ref,
-                  cnt, wb1, wb3, wb2, xfew, xall, csem, wsem, dsem, xsem):
+def hidden_kernel(cnt_hbm, xg_hbm, w1_hbm, w3_hbm, pre1, pre3, pre2, h_ref,
+                  cnt, wb1, wb3, xfew, xall, csem, wsem, xsem):
     n_exp, d_model, ff = w1_hbm.shape
     nd = cnt.shape[0]
     depth = wb1.shape[0]
@@ -327,15 +330,8 @@
         def _():
             all_copy(e).start()
 
-    early_w = wb2.shape[2]
-
-    def dcopy(e):
-        return pltpu.make_async_copy(w2_hbm.at[e, :, pl.ds(0, early_w)], wb2.at[e % 2], dsem.at[e % 2])
-
     ccopy = pltpu.make_async_copy(cnt_hbm, cnt, csem)
     ccopy.start()
-    dcopy(0).start()
-    dcopy(1).start()
     for e in range(first, first + depth):
         for j in range(len(groups)):
             for c in wcopy(e, e % depth, j):
@@ -354,8 +350,8 @@
 
     def down(e, slots):
         rows = h_ref[e, :, 0:slots, 0:ff].reshape(nd * slots, ff)
-        for c0 in range(0, early_w, 256):
-            out = jnp.dot(rows, wb2[e % 2, :, c0:c0 + 256], preferred_element_type=F32)
+        for c0 in range(0, pre2.shape[2], 256):
+            out = jnp.dot(rows, pre2[e, :, c0:c0 + 256], preferred_element_type=F32)
             h_ref[e, :, 0:slots, ff + c0:ff + c0 + 256] = out.astype(BF16).reshape(nd, slots, 256)
 
     def expert(e, gate, up, wait, refill):
@@ -369,7 +365,6 @@
                 for c0, w in cols:
                     h_ref[e, :, 0:FEW, c0:c0 + w] = hidden(xfew.at[e % 2], up, gate, c0, w)
                 refill(j)
-            dcopy(e).wait()
             down(e, FEW)
 
         @pl.when(jnp.logical_not(small))
@@ -380,13 +375,11 @@
                 for c0, w in cols:
                     h_ref[e, :, :, c0:c0 + w] = hidden(xall.at[e % 2], up, gate, c0, w)
                 refill(j)
-            dcopy(e).wait()
             down(e, SLOT)
 
         @pl.when(e + 2 < n_exp)
         def _():
             rows_start(e + 2)
-            dcopy(e + 2).start()
 
     def early(e, carry):
         expert(e, pre1.at[e], pre3.at[e], lambda j: None, lambda j: None)
@@ -412,7 +405,7 @@
     lax.fori_loop(first, n_exp, late, 0)
 
 
-def hidden_call(cnt, xg, w1, w3, w2, pre1, pre3):
+def hidden_call(cnt, xg, w1, w3, pre1, pre3, pre2):
     n_exp, d_model, ff = w1.shape
     nd = cnt.shape[0]
     depth = 2
@@ -422,21 +415,21 @@
     return pl.pallas_call(
         hidden_kernel,
         out_shape=pltpu.VMEM((n_exp, nd, SLOT, ff + EARLY * CHUNK), BF16),
-        in_specs=[any_spec] * 5 + [vmem, vmem],
+        in_specs=[any_spec] * 4 + [vmem] * 3,
         out_specs=vmem,
         scratch_shapes=[
             pltpu.SMEM(cnt.shape, jnp.int32),
             pltpu.VMEM((depth, d_model, ff), BF16),
             pltpu.VMEM((depth, d_model, ff), BF16),
-            pltpu.VMEM((2, ff, EARLY * CHUNK), BF16),
             pltpu.VMEM((2, nd, FEW, d_model), BF16),
             pltpu.VMEM((2, nd, SLOT, d_model), BF16),
-            dma(()), dma((depth, 2, 2)), dma((2,)), dma((2,)),
+            dma(()), dma((depth, 2, 2)), dma((2,)),
         ],
-        compiler_params=pltpu.CompilerParams(vmem_limit_bytes=33_800_000),
+        compiler_params=pltpu.CompilerParams(vmem_limit_bytes=29_500_000),
         name="routed_hidden",
-    )(cnt, xg, w1, w3, w2, pltpu.with_memory_space_constraint(pre1, pltpu.VMEM),
-      pltpu.with_memory_space_constraint(pre3, pltpu.VMEM))
+    )(cnt, xg, w1, w3, pltpu.with_memory_space_constraint(pre1, pltpu.VMEM),
+      pltpu.with_memory_space_constraint(pre3, pltpu.VMEM),
+      pltpu.with_memory_space_constraint(pre2, pltpu.VMEM))
 
 
 def down_kernel(hv, g_hbm, hsh_hbm, w2_hbm, sd_hbm, y_hbm,
@@ -675,8 +668,8 @@
     nd = mesh.shape["ep"]
 
     def device_fn(x, route, gates, w_gate, w_up, w_down, sg, su, sd):
-        xg, hsh, cnt, g, pre1, pre3 = gather_call(x, route.T, gates.T, sg, su, w_gate, w_up, nd)
-        h = hidden_call(cnt, xg, w_gate, w_up, w_down, pre1, pre3)
+        xg, hsh, cnt, g, *pre = gather_call(x, route.T, gates.T, sg, su, w_gate, w_up, w_down, nd)
+        h = hidden_call(cnt, xg, w_gate, w_up, *pre)
         return down_call(h.reshape(h.shape[0], -1, h.shape[3]), g, hsh, w_down, sd)
 
     tok = P(("dp", "ep"), None)

time: 96.9 us -> 98.7 us (1.019); the launches traced: 95.6 us -> 98.4 us
  Pallas kernels: 93.8 us -> 96.6 us
    pallas_call x1, Pallas kernels: 36.8 us -> 41.2 us  [down_call(): pl.pallas_call(down_kernel, out_shape=jax.ShapeDtypeStruct((rows, d_model...]
    pallas_call x1, Pallas kernels: 34.1 us -> 30.9 us  [hidden_call(): pl.pallas_call(hidden_kernel, out_shape=pltpu.VMEM((n_exp, nd, SLOT, ff +...]
    pallas_call x1, Pallas kernels: 22.8 us -> 24.5 us  [gather_call(): pl.pallas_call(gather_kernel, out_shape=(jax.ShapeDtypeStruct((8, nd, SLO...]
where the time goes in v5:
time: 98.7 us; the launch traced here: 98.4 us
  Pallas kernels  96.6 us (98%)
  local copies, waits for them, and re-layouts  1.77 us (2%)
    pallas_call x1, Pallas kernels, down_call(): pl.pallas_call(down_kernel, out_shape=jax.ShapeDtypeStruct((rows, d_model...  41.2 us
    pallas_call x1, Pallas kernels, hidden_call(): pl.pallas_call(hidden_kernel, out_shape=pltpu.VMEM((n_exp, nd, SLOT, ff +...  30.9 us
    pallas_call x1, Pallas kernels, gather_call(): pl.pallas_call(gather_kernel, out_shape=(jax.ShapeDtypeStruct((8, nd, SLO...  24.5 us

profile of v5, /device:TPU:0, one launch (start us, length us, event | category | flops | bytes accessed | tf_op | source)
XLA Modules:
  0.0 98.4 jit_solution(8610102920752673586)
XLA Ops:
  0.0 24.5 %gather_shared.1 = (bf16[8,8,40,2048]{3,2,1,0:T(8,128)(2,1)}, bf16[96,2816]{1,0:T(8,128)(2,1)}, s32[8,8,128]{2,1,0:T(8,128)}, bf16[8,288,320]{2,1,0:T(8,128)(2,1...) custom-call(bf16[96,2048]{1,0:T(8,128)(2,1)} %x_hbm.1, ...), custom_call_target="tpu_custom_call" | custom-call | tf_op jit(solution)/shard_map/gather_shared/pallas_call | solution.py:257
  24.5 30.9 %routed_hidden.1 = bf16[8,8,40,1664]{3,2,1,0:T(8,128)(2,1)S(1)} custom-call(s32[8,8,128]{2,1,0:T(8,128)} %get-tuple-element.12.cnt_hbm, bf16[8,8,40,2048]{3,2,1,0:T(8,128)(2,1)} %get-tuple-element.13.xg_hbm, bf16[8,2048,1408]{2,1,0:T(8,128)(2,1)} %w1_hbm.3, bf16[8,2048,1408]{2,1,0:T(8,128)(2,1)} %w3_hbm.3, ...), custom_call_target="tpu_custom_call" | custom-call | tf_op jit(solution)/shard_map/routed_hidden/pallas_call | solution.py:415
  55.4 41.2 %down_reduce.1 = bf16[96,2048]{1,0:T(8,128)(2,1)} custom-call(bf16[8,320,1664]{2,1,0:T(8,128)(2,1)S(1)} %bitcast.3, bf16[8,288,320]{2,1,0:T(8,128)(2,1)} %get-tuple-element.17.g_hbm, bf16[96,2816]{1,0:T(8,128)(2,1)} %get-tuple-element.18.hsh_hbm, bf16[8,1408,2048]{2,1,0:T(8,128)(2,1)} %w2_hbm.3, bf16[2816,2048]{1,0:T(8,128)(2,1)} %sd_hbm.1), custom_call_target="tpu_custom_call" | custom-call | tf_op jit(solution)/shard_map/down_reduce/pallas_call | solution.py:640
  96.7 1.8 %copy.11 = bf16[96,2048]{1,0:T(8,128)(2,1)} copy(bf16[96,2048]{1,0:T(8,128)(2,1)} %down_reduce.1) | data formatting | bytes 786432

commit v6 on v5

--- a/solution.py
+++ b/solution.py
@@ -13,7 +13,7 @@
 VMEM_LIMIT = 67_000_000
 H_BYTES = 10_500_000
 CHUNK = 256
-GROUP = 4
+GROUP = 8
 EARLY = 1
 PRE = 2
 PRE_BYTES = 23_500_000
@@ -294,7 +294,7 @@
 FEW = 16
 
 
-def hidden_kernel(cnt_hbm, xg_hbm, w1_hbm, w3_hbm, pre1, pre3, pre2, h_ref,
+def hidden_kernel(cnt_hbm, xg_hbm, w1_hbm, w3_hbm, in1, in3, pre2, h_ref, pre1, pre3,
                   cnt, wb1, wb3, xfew, xall, csem, wsem, xsem):
     n_exp, d_model, ff = w1_hbm.shape
     nd = cnt.shape[0]
@@ -304,10 +304,13 @@
     cut = 3 * 256
     groups = ((0, cut, bounds[:3]), (cut, ff - cut, bounds[3:]))
 
-    def wcopy(e, slot, j):
+    def wcopy(e, late, j):
         c0, w, _ = groups[j]
-        return (pltpu.make_async_copy(w1_hbm.at[e, :, c0:c0 + w], wb1.at[slot, :, c0:c0 + w], wsem.at[slot, 0, j]),
-                pltpu.make_async_copy(w3_hbm.at[e, :, c0:c0 + w], wb3.at[slot, :, c0:c0 + w], wsem.at[slot, 1, j]))
+        d1, d3 = (wb1, wb3) if late else (pre1, pre3)
+        slot = e % depth
+        sem = slot + depth if late else slot
+        return (pltpu.make_async_copy(w1_hbm.at[e, :, c0:c0 + w], d1.at[slot, :, c0:c0 + w], wsem.at[sem, 0, j]),
+                pltpu.make_async_copy(w3_hbm.at[e, :, c0:c0 + w], d3.at[slot, :, c0:c0 + w], wsem.at[sem, 1, j]))
 
     def few(e):
         top = cnt[0, e, 0]
@@ -334,7 +337,7 @@
     ccopy.start()
     for e in range(first, first + depth):
         for j in range(len(groups)):
-            for c in wcopy(e, e % depth, j):
+            for c in wcopy(e, True, j):
                 c.start()
     ccopy.wait()
     rows_start(0)
@@ -381,28 +384,34 @@
         def _():
             rows_start(e + 2)
 
-    def early(e, carry):
-        expert(e, pre1.at[e], pre3.at[e], lambda j: None, lambda j: None)
+    def stretch(start, late):
+        def body(k, carry):
+            e = start + k
+            d1, d3 = (wb1, wb3) if late else (pre1, pre3)
+
+            def wait(j):
+                @pl.when(e >= first)
+                def _():
+                    for c in wcopy(e, late, j):
+                        c.wait()
+
+            def refill(j):
+                @pl.when(e + 2 * depth < n_exp)
+                def _():
+                    for c in wcopy(e + 2 * depth, late, j):
+                        c.start()
+
+            expert(e, d1.at[k], d3.at[k], wait, refill)
+            return carry
+
+        lax.fori_loop(0, depth, body, 0)
+
+    def both(i, carry):
+        stretch(2 * depth * i, False)
+        stretch(2 * depth * i + depth, True)
         return carry
 
-    def late(e, carry):
-        slot = e % depth
-
-        def wait(j):
-            for c in wcopy(e, slot, j):
-                c.wait()
-
-        def refill(j):
-            @pl.when(e + depth < n_exp)
-            def _():
-                for c in wcopy(e + depth, slot, j):
-                    c.start()
-
-        expert(e, wb1.at[slot], wb3.at[slot], wait, refill)
-        return carry
-
-    lax.fori_loop(0, first, early, 0)
-    lax.fori_loop(first, n_exp, late, 0)
+    lax.fori_loop(0, n_exp // (2 * depth), both, 0)
 
 
 def hidden_call(cnt, xg, w1, w3, pre1, pre3, pre2):
@@ -414,22 +423,24 @@
     dma = pltpu.SemaphoreType.DMA
     return pl.pallas_call(
         hidden_kernel,
-        out_shape=pltpu.VMEM((n_exp, nd, SLOT, ff + EARLY * CHUNK), BF16),
+        out_shape=(pltpu.VMEM((n_exp, nd, SLOT, ff + EARLY * CHUNK), BF16),
+                   pltpu.VMEM(pre1.shape, BF16), pltpu.VMEM(pre3.shape, BF16)),
+        input_output_aliases={4: 1, 5: 2},
         in_specs=[any_spec] * 4 + [vmem] * 3,
-        out_specs=vmem,
+        out_specs=(vmem,) * 3,
         scratch_shapes=[
             pltpu.SMEM(cnt.shape, jnp.int32),
             pltpu.VMEM((depth, d_model, ff), BF16),
             pltpu.VMEM((depth, d_model, ff), BF16),
             pltpu.VMEM((2, nd, FEW, d_model), BF16),
             pltpu.VMEM((2, nd, SLOT, d_model), BF16),
-            dma(()), dma((depth, 2, 2)), dma((2,)),
+            dma(()), dma((2 * depth, 2, 2)), dma((2,)),
         ],
         compiler_params=pltpu.CompilerParams(vmem_limit_bytes=29_500_000),
         name="routed_hidden",
     )(cnt, xg, w1, w3, pltpu.with_memory_space_constraint(pre1, pltpu.VMEM),
       pltpu.with_memory_space_constraint(pre3, pltpu.VMEM),
-      pltpu.with_memory_space_constraint(pre2, pltpu.VMEM))
+      pltpu.with_memory_space_constraint(pre2, pltpu.VMEM))[0]
 
 
 def down_kernel(hv, g_hbm, hsh_hbm, w2_hbm, sd_hbm, y_hbm,

time: 98.7 us -> 98.1 us (level)
  no operation moved by 1% of the time
where the time goes in v6:
time: 98.1 us; the launch traced here: 98.3 us
  Pallas kernels  96.5 us (98%)
  local copies, waits for them, and re-layouts  1.77 us (2%)
    pallas_call x1, Pallas kernels, down_call(): pl.pallas_call(down_kernel, out_shape=jax.ShapeDtypeStruct((rows, d_model...  40.9 us
    pallas_call x1, Pallas kernels, hidden_call(): pl.pallas_call(hidden_kernel, out_shape=(pltpu.VMEM((n_exp, nd, SLOT, ff...  31.1 us
    pallas_call x1, Pallas kernels, gather_call(): pl.pallas_call(gather_kernel, out_shape=(jax.ShapeDtypeStruct((8, nd, SLO...  24.5 us

profile of v6, /device:TPU:0, one launch (start us, length us, event | category | flops | bytes accessed | tf_op | source)
XLA Modules:
  0.0 98.3 jit_solution(11457572640681302305)
XLA Ops:
  0.0 24.5 %gather_shared.1 = (bf16[8,8,40,2048]{3,2,1,0:T(8,128)(2,1)}, bf16[96,2816]{1,0:T(8,128)(2,1)}, s32[8,8,128]{2,1,0:T(8,128)}, bf16[8,288,320]{2,1,0:T(8,128)(2,1...) custom-call(bf16[96,2048]{1,0:T(8,128)(2,1)} %x_hbm.1, ...), custom_call_target="tpu_custom_call" | custom-call | tf_op jit(solution)/shard_map/gather_shared/pallas_call | solution.py:257
  24.5 31.1 %routed_hidden.1 = (bf16[8,8,40,1664]{3,2,1,0:T(8,128)(2,1)S(1)}, bf16[2,2048,1408]{2,1,0:T(8,128)(2,1)S(1)}, bf16[2,2048,1408]{2,1,0:T(8,128)(2,1)S(1)}) custom-call(s32[8,8,128]{2,1,0:T(8,128)} %get-tuple-element.13.cnt_hbm, bf16[8,8,40,2048]{3,2,1,0:T(8,128)(2,1)} %get-tuple-element.14.xg_hbm, ...), custom_call_target="tpu_custom_call", output_to_operand_aliasing={{1}: (4, {}), {2}: (5, {})} | custom-call | tf_op jit(solution)/shard_map/routed_hidden/pallas_call | solution.py:424
  55.6 40.9 %down_reduce.1 = bf16[96,2048]{1,0:T(8,128)(2,1)} custom-call(bf16[8,320,1664]{2,1,0:T(8,128)(2,1)S(1)} %bitcast.3, bf16[8,288,320]{2,1,0:T(8,128)(2,1)} %get-tuple-element.19.g_hbm, bf16[96,2816]{1,0:T(8,128)(2,1)} %get-tuple-element.20.hsh_hbm, bf16[8,1408,2048]{2,1,0:T(8,128)(2,1)} %w2_hbm.3, bf16[2816,2048]{1,0:T(8,128)(2,1)} %sd_hbm.1), custom_call_target="tpu_custom_call" | custom-call | tf_op jit(solution)/shard_map/down_reduce/pallas_call | solution.py:651
  96.5 1.8 %copy.15 = bf16[96,2048]{1,0:T(8,128)(2,1)} copy(bf16[96,2048]{1,0:T(8,128)(2,1)} %down_reduce.1) | data formatting | bytes 786432
